TPU v7x, 256 devices: a whole 4x4x8 slice. The times are simulated.
256 devices in a mesh: aa: 8 (over y, core), ba: 4 (over x), col: 8 (over z).
Axes of the slice: x: 4, y: 4, z: 8, core: 2. Of those that a mesh axis runs over, the one named last changes fastest.
Arguments:
- hidden: bfloat16 [8, 4, 32, 8192], P('aa', 'ba', None, 'col'), may hold values from -36 to 60, as said below
- unembed: bfloat16 [8192, 152064], P(None, ('aa', 'ba', 'col')), may hold values from -1 to 5, as said below
- targets: int32 [8, 4, 32], replicated, may hold values from 0 to 152063
- lengths: int32 [8, 4], replicated, may hold values from 1 to 32
Outputs:
- scores: float32 [8, 4], P('aa', 'ba')
Inputs may be any that keep to these rules, and one draw needn't show every extreme that they name: real-valued hidden states. `unembed`: real-valued unembedding entries.
All inputs are finite; a program needn't handle non-finite values.
Results may differ from a plain program's by a relative error of at most 0.0003.
Values may be sent and summed in bfloat16 or wider, within the bound.
A program may use at most 128 MiB of HBM per device.

v0:
```python
import jax
import jax.numpy as jnp
from jax import lax
from jax.sharding import Mesh
from jax.sharding import PartitionSpec as P

AA = ("aa_0", "aa_1")
AA_BA_COL = ("aa_0", "aa_1", "ba", "col")
AA_BA = ("aa_0", "aa_1", "ba")


def in_order(parts, dim):
    parts = jnp.moveaxis(parts, 0, dim)
    dims = parts.shape
    return parts.reshape(*dims[:dim], dims[dim] * dims[dim + 1], *dims[dim + 2 :])


def copy_for_each(x, axis):
    copies = jnp.broadcast_to(x, (lax.axis_size(axis), *x.shape))
    return lax.all_to_all(copies, axis, split_axis=0, concat_axis=0, tiled=True)


def gather_directly(x, axis, dim):
    return in_order(copy_for_each(x, axis), dim)


def gathered_once(x, axis):
    leaves = jax.tree.leaves(x)
    turns = sorted(range(len(leaves)), key=lambda k: -leaves[k].size)
    width = (1, *leaves[turns[0]].shape)[-1]
    lines = [
        jnp.pad(leaves[k].reshape(-1), (0, -leaves[k].size % width)).reshape(-1, width)
        for k in turns
    ]
    both, at, found = (lax.all_gather(jnp.concatenate(lines), axis), 0, {})
    for k, line in zip(turns, lines):
        slab = both[:, at : at + len(line)].reshape(len(both), -1)
        found[k] = slab[:, : leaves[k].size].reshape(-1, *leaves[k].shape)
        at += len(line)
    numbers = iter(range(len(leaves)))
    return jax.tree.map(lambda _: found[next(numbers)], x)


def merged_by_axis(x, axes, combine):
    for axis in axes:
        pieces = gathered_once(x, axis)
        x = jax.tree.map(lambda part: part[0], pieces)
        for k in range(1, lax.axis_size(axis)):
            x = combine(x, jax.tree.map(lambda part: part[k], pieces))
    return x


def combine_stats(earlier, later):
    top_one, total_one, picked_one = earlier
    top_two, total_two, picked_two = later
    joined = jnp.maximum(top_one, top_two)
    total = total_one * jnp.exp(top_one - joined) + total_two * jnp.exp(top_two - joined)
    return (joined, total, picked_one + picked_two)


def body(hidden, unembed, targets, lengths):
    groups = lax.axis_size(AA)
    members = lax.axis_size("ba")
    per_group, choices_dev, seq_len, width_part = hidden.shape
    block_rows = per_group * choices_dev * seq_len
    own_rows = hidden.reshape(block_rows, width_part)
    vocab_part = unembed.shape[1]
    device_index = lax.axis_index(AA_BA_COL)
    offset = device_index * vocab_part
    full_rows = gather_directly(own_rows, "col", 1)
    logits = jnp.dot(
        lax.all_gather(full_rows, AA_BA, axis=0, tiled=True),
        unembed,
        preferred_element_type=jnp.float32,
    )
    ordered = targets.reshape(groups, per_group, members, seq_len).transpose(0, 2, 1, 3).reshape(-1)
    local_ids = ordered - offset
    columns = jnp.arange(vocab_part, dtype=jnp.int32)
    picked_part = jnp.sum(jnp.where(local_ids[:, None] == columns[None, :], logits, 0.0), axis=1)
    group_index = lax.axis_index(AA)
    member_index = lax.axis_index("ba")
    own_len = lax.dynamic_slice(lengths, (group_index * per_group, member_index), (per_group, 1))
    positions = jnp.arange(seq_len, dtype=jnp.int32)
    local_top = jnp.max(logits, axis=1)
    relative = jnp.sum(jnp.exp(logits - local_top[:, None]), axis=1)
    top, total, picked = merged_by_axis(
        (local_top, relative, picked_part), AA_BA_COL, combine_stats
    )
    first = (group_index * members + member_index) * block_rows
    mine = lax.dynamic_slice_in_dim(picked - top - jnp.log(total), first, block_rows).reshape(
        per_group, seq_len
    )
    valid = positions[None, :] < own_len
    summed = jnp.sum(jnp.where(valid, mine, 0.0), axis=1)
    return (summed / own_len[:, 0].astype(jnp.float32))[:, None]


def solution(mesh):
    split = Mesh(
        mesh.devices.reshape(4, 2, mesh.shape["ba"], mesh.shape["col"]),
        ("aa_0", "aa_1", "ba", "col"),
    )
    in_specs = (P(AA, "ba", None, "col"), P(None, AA_BA_COL), P(), P())
    out_specs = P(AA, "ba")
    return jax.shard_map(body, mesh=split, in_specs=in_specs, out_specs=out_specs, check_vma=False)
```

profile of v0, /device:TPU:2, one launch (start us, length us, event | category | flops | bytes accessed | tf_op | source)
XLA Modules:
  0.0 185.8 jit_solution(12175652836842939492)
XLA Ops:
  6.5 0.0 copy-start
  6.5 0.0 all-gather.10.cloned.1.call-start
  6.5 0.9 broadcast_in_dim.18
  7.4 25.8 %all_to_all.5 = bf16[8,32,1024]{2,1,0:T(8,128)(2,1)S(1)} all-to-all(bf16[8,32,1024]{2,1,0:T(8,128)(2,1)S(1)} %broadcast_in_dim.18), channel_id=1, replica_groups=mesh['aa_0'=4,'aa_1'=2,'ba'=4,'col'=8] {'col'}, dimensions={0} | all-to-all | bytes 1048576 | tf_op jit(solution)/shard_map/all_to_all | solution.py:20
  33.2 0.8 copy.6
  34.0 0.0 all-gather.10.cloned.1.call-update
  34.1 0.0 copy-done
  34.1 0.1 sub.213
  34.2 1.3 dynamic_slice.6
  36.1 72.0 %all-gather.10.cloned.1.call-done = bf16[1024,8192]{1,0:T(8,128)(2,1)} async-done(((bf16[32,8192]{1,0:T(8,128)(2,1)}), bf16[1024,8192]{1,0:T(8,128)(2,1)}) %all-gather.10.cloned.1.call-update) | async-done | bytes 16777232 | tf_op jit(solution)/shard_map/all_gather | solution.py:72
  108.1 15.5 %fusion.49 = (f32[1024]{0:T(1024)S(1)}, f32[1024,594]{0,1:T(8,128)S(1)}) fusion(bf16[1024,8192]{1,0:T(8,128)(2,1)} %all-gather.10.cloned.1.call-done, bf16[8192,594]{0,1:T(8,128)(2,1)} %param.5), kind=kOutput, calls=%fused_computation.97 | convolution fusion | flops 9966273536 | bytes 28946432 | tf_op jit(solution)/shard_map/dot_general | solution.py:71
  123.6 0.7 exponential_reduce_fusion
  124.3 11.9 %all-gather.4 = f32[4,3,1024]{2,1,0:T(4,128)S(1)} all-gather(f32[1,3,1024]{2,1,0:T(4,128)S(1)} %maximum_bitcast_fusion), channel_id=2, replica_groups=mesh['aa_0'=4,'aa_1'=2,'ba'=4,'col'=8] {'aa_0'}, dimensions={0}, use_global_device_ids=true | all-gather | bytes 61440 | tf_op jit(solution)/shard_map/all_gather | solution.py:35
  136.2 0.1 fusion.16
  136.3 1.8 all-gather.5
  138.2 11.8 %all-gather.6 = f32[4,3,1024]{2,1,0:T(4,128)S(1)} all-gather(f32[1,3,1024]{2,1,0:T(4,128)S(1)} %maximum_bitcast_fusion.2), channel_id=4, replica_groups=mesh['aa_0'=4,'aa_1'=2,'ba'=4,'col'=8] {'ba'}, dimensions={0}, use_global_device_ids=true | all-gather | bytes 61440 | tf_op jit(solution)/shard_map/all_gather | solution.py:35
  150.1 0.1 fusion.2
  150.2 26.1 %all-gather.7 = f32[8,3,1024]{2,1,0:T(4,128)S(1)} all-gather(f32[1,3,1024]{2,1,0:T(4,128)S(1)} %maximum_bitcast_fusion.3), channel_id=5, replica_groups=mesh['aa_0'=4,'aa_1'=2,'ba'=4,'col'=8] {'col'}, dimensions={0}, use_global_device_ids=true | all-gather | bytes 110592 | tf_op jit(solution)/shard_map/all_gather | solution.py:35
  176.2 0.1 fusion.47
  176.3 1.4 fusion.43
  (11 shorter events, 0.2 us)
Async XLA Ops:
  6.5 27.5 %copy-start = (s32[8,4,32]{2,1,0:T(4,128)S(1)}, s32[8,4,32]{2,1,0:T(4,128)}, u32[]{:S(2)}) copy-start(s32[8,4,32]{2,1,0:T(4,128)} %param.6) | copy-start | bytes 12292
  6.5 101.5 %all-gather.10.cloned.1.call-start = ((), (), s32[]{:S(2)}) async-start(), calls=%async_computation.1 | async-start | bytes 17301504 | tf_op jit(solution)/shard_map/all_gather | solution.py:72
Sparse Core Ops, SparseCore 0:
  34.2 73.8 all-gather.9
where the time goes:
time: 186 us
  blocking collectives  77.4 us (42%)
  waiting for transfers between devices  72 us (39%)
  matrix products  15.5 us (8%)
  between operations  15.4 us (8%)
  local copies, waits for them, and re-layouts  3.1 us (2%)
  other arithmetic  2.39 us (1%)
    all_gather x1, waiting for transfers between devices, body(): lax.all_gather(full_rows, AA_BA, axis=0, tiled=True)  72 us
    all_gather x4, blocking collectives, gathered_once(): both, at, found = (lax.all_gather(jnp.concatenate(lines), axis), 0, {})  51.6 us
    all_to_all x1, blocking collectives, copy_for_each(): return lax.all_to_all(copies, axis, split_axis=0, concat_axis=0, tiled=True)  25.8 us
    dot_general x1, matrix products, body(): jnp.dot(lax.all_gather(full_rows, AA_BA, axis=0, tiled=True), unembed, pr...  15.5 us
  transfers between devices with their start and end apart: 1, of which 1 were waited for; matrix products, arithmetic and copies ran while one was open for 1% of the time, Pallas kernels for 0%

commit v1 on v0

v1 whole, which is shorter than its diff:
```python
import functools

import jax
import jax.numpy as jnp
from jax import lax
from jax.experimental import pallas as pl
from jax.experimental.pallas import tpu as pltpu
from jax.sharding import PartitionSpec as P

MESH = pl.DeviceIdType.MESH
NX, NY, NZ, NC = 4, 4, 8, 2
SEQ = 32
WIDE, THIN = 768, 256
WAVES = NZ
BF16, F32 = jnp.bfloat16, jnp.float32


def kernel(
    hid, unembed, targets, lengths, out,
    hab, hc, ub, acc, tcol, stat, gath, zst,
    own_sem, usem, zr, zs, pr, ps, tr, ts, dr, ds, cr, cs, er, es,
):
    aa, x, z = lax.axis_index("aa"), lax.axis_index("ba"), lax.axis_index("col")
    y, c = aa // 2, aa % 2
    vocab = unembed.shape[1]
    other = 1 - c

    def at(xx, yy, zz, cc):
        return {"aa": yy * 2 + cc, "ba": xx, "col": zz}

    xp, xm = (x + 1) % NX, (x + NX - 1) % NX
    yp, ym = (y + 1) % NY, (y + NY - 1) % NY
    zp, zm = (z + 1) % NZ, (z + NZ - 1) % NZ
    to_xp, to_xm = at(xp, y, z, c), at(xm, y, z, c)
    to_yp, to_ym = at(x, yp, z, c), at(x, ym, z, c)
    to_zp, to_zm = at(x, y, zp, c), at(x, y, zm, c)
    partner = at(x, y, z, other)

    def copy(src, dst, ssem, rsem, dev):
        return pltpu.make_async_remote_copy(
            src_ref=src, dst_ref=dst, send_sem=ssem, recv_sem=rsem, device_id=dev, device_id_type=MESH
        )

    def push(ref, ssem, rsem, dev):
        copy(ref, ref, ssem, rsem, dev).start()

    def got(ref, ssem, rsem):
        copy(ref, ref, ssem, rsem, partner).wait_recv()

    def sent(ref, ssem, rsem):
        copy(ref, ref, ssem, rsem, partner).wait_send()

    wide_in = pltpu.make_async_copy(
        hid.at[0, 0, :, pl.ds(0, WIDE)], hab.at[z, c, x, y], own_sem.at[0])
    thin_in = pltpu.make_async_copy(
        hid.at[0, 0, :, pl.ds(WIDE, THIN)], hc.at[z, c, x, y], own_sem.at[1])
    wide_in.start()
    thin_in.start()

    def weights(k):
        return pltpu.make_async_copy(
            unembed.at[pl.ds(k * 1024, 1024), :], ub.at[k], usem.at[k])

    barrier = pltpu.get_barrier_semaphore()
    for dev in (to_xp, to_xm, to_yp, to_ym, to_zp, to_zm, partner):
        pl.semaphore_signal(barrier, inc=1, device_id=dev, device_id_type=MESH)
    wide_in.wait()
    thin_in.wait()
    pl.semaphore_wait(barrier, 7)

    def s1(b, zz, wa, w):
        s, r = ps.at[w, 0], pr.at[w, 0]
        one = b.at[zz, c, x, y, :, pl.ds(0, wa)]
        two = b.at[zz, c, x, y, :, pl.ds(wa, wa)]
        push(one, s, r, to_yp)
        push(two, s, r, to_xp)
        push(one, s, r, to_ym)
        push(two, s, r, to_xm)

    def s2(b, zz, wa, w):
        got(b.at[zz, c, x, :, :, pl.ds(0, wa)], ps.at[w, 0], pr.at[w, 0])
        s, r = ps.at[w, 1], pr.at[w, 1]
        push(b.at[zz, c, x, ym, pl.ds(0, 16), pl.ds(0, wa)], s, r, to_yp)
        push(b.at[zz, c, xm, y, pl.ds(0, 16), pl.ds(wa, wa)], s, r, to_xp)
        push(b.at[zz, c, x, yp, pl.ds(16, 16), pl.ds(0, wa)], s, r, to_ym)
        push(b.at[zz, c, xp, y, pl.ds(16, 16), pl.ds(wa, wa)], s, r, to_xm)

    def s3(b, zz, wa, w):
        got(b.at[zz, c, x, pl.ds(0, 2), :, pl.ds(0, wa)], ps.at[w, 1], pr.at[w, 1])
        s, r = ps.at[w, 2], pr.at[w, 2]
        one = b.at[zz, c, x, :, :, pl.ds(0, wa)]
        two = b.at[zz, c, :, y, :, pl.ds(wa, wa)]
        push(one, s, r, to_xp)
        push(two, s, r, to_yp)
        push(one, s, r, to_xm)
        push(two, s, r, to_ym)

    def s4(b, zz, wa, w):
        got(b.at[zz, c, :, :, :, pl.ds(0, wa)], ps.at[w, 2], pr.at[w, 2])
        s, r = ps.at[w, 3], pr.at[w, 3]
        push(b.at[zz, c, xm, pl.ds(0, 2), :, pl.ds(0, wa)], s, r, to_xp)
        push(b.at[zz, c, pl.ds(0, 2), ym, :, pl.ds(wa, wa)], s, r, to_yp)
        push(b.at[zz, c, xp, pl.ds(2, 2), :, pl.ds(0, wa)], s, r, to_xm)
        push(b.at[zz, c, pl.ds(2, 2), yp, :, pl.ds(wa, wa)], s, r, to_ym)

    def s5(b, zz, wa, w):
        got(b.at[zz, c, pl.ds(0, 2), :, :, pl.ds(0, wa)], ps.at[w, 3], pr.at[w, 3])

    def s_done(b, wa, w):
        sent(b.at[0, 0, 0, :, :, pl.ds(0, wa)], ps.at[w, 0], pr.at[w, 0])
        sent(b.at[0, 0, 0, pl.ds(0, 2), :, pl.ds(0, wa)], ps.at[w, 1], pr.at[w, 1])
        sent(b.at[0, 0, :, :, :, pl.ds(0, wa)], ps.at[w, 2], pr.at[w, 2])
        sent(b.at[0, 0, pl.ds(0, 2), :, :, pl.ds(0, wa)], ps.at[w, 3], pr.at[w, 3])

    def slot(j):
        k = (j + 1) // 2
        return (z + NZ + k * (1 - 2 * (j % 2))) % NZ

    LAST = WAVES
    wa, wc = WIDE // 2, THIN // 2

    def z_in(j):
        got(hab.at[slot(j), c, x, y], zs.at[j], zr.at[j])

    def z_on(j):
        @pl.when(j == 0)
        def _():
            push(hab.at[z, c, x, y], zs.at[1], zr.at[1], to_zp)
            push(hab.at[z, c, x, y], zs.at[2], zr.at[2], to_zm)

        @pl.when((j % 2 == 1) & (j < WAVES - 1))
        def _():
            push(hab.at[slot(j), c, x, y], zs.at[j + 2], zr.at[j + 2], to_zp)

        @pl.when((j % 2 == 0) & (j > 0) & (j < WAVES - 2))
        def _():
            push(hab.at[slot(j), c, x, y], zs.at[j + 2], zr.at[j + 2], to_zm)

    def t1():
        for q in range(2):
            mine = hc.at[z, c, pl.ds(2 * q, 2)]
            push(mine, ts.at[0, q], tr.at[0, q], to_zp)
            push(mine, ts.at[0, q], tr.at[0, q], to_zm)

    def t_in(k, q):
        got(hc.at[z, c], ts.at[k - 1, q], tr.at[k - 1, q])

    def t_step(k, q):
        t_in(k, q)
        below, above = (z + NZ - k) % NZ, (z + k) % NZ
        if k < 3:
            push(hc.at[below, c, pl.ds(2 * q, 2)], ts.at[k, q], tr.at[k, q], to_zp)
            push(hc.at[above, c, pl.ds(2 * q, 2)], ts.at[k, q], tr.at[k, q], to_zm)
        elif q == 0:
            push(hc.at[below, c, pl.ds(0, 2)], ts.at[3, 0], tr.at[3, 0], to_zp)
        else:
            push(hc.at[above, c, pl.ds(2, 2)], ts.at[3, 0], tr.at[3, 0], to_zm)

    def thin_over(k):
        push(hc.at[(z + NZ - k) % NZ, c], cs.at[k], cr.at[k], partner)
        if 0 < k < 4:
            push(hc.at[(z + k) % NZ, c], cs.at[k], cr.at[k], partner)

    def thin_bytes(k):
        return hc.at[0] if 0 < k < 4 else hc.at[0, 0]

    def multiply(b, zz, k0, kw):
        @pl.loop(0, NC)
        def _(h):
            lhs = b[zz, h].reshape(NX * NY * SEQ, kw)
            rhs = ub[zz, pl.ds(k0, kw), :]
            rows = pl.ds(pl.multiple_of(h * 512, 512), 512)
            acc[rows, :] += jnp.dot(lhs, rhs, preferred_element_type=F32)

    def thin_multiply(k):
        got(thin_bytes(k), cs.at[k], cr.at[k])
        multiply(hc, (z + NZ - k) % NZ, WIDE, THIN)
        if 0 < k < 4:
            multiply(hc, (z + k) % NZ, WIDE, THIN)

    s1(hc, z, wc, LAST)
    z_on(0)
    s1(hab, z, wa, 0)

    for k in range(NZ):
        weights(k).start()
    acc[...] = jnp.zeros_like(acc)
    eye = lax.broadcasted_iota(jnp.int32, (SEQ, SEQ), 0) == lax.broadcasted_iota(jnp.int32, (SEQ, SEQ), 1)
    for cc in range(NC):
        for xx in range(NX):
            for yy in range(NY):
                row = targets[2 * yy + cc, pl.ds(xx, 1), :].astype(F32)
                col = jnp.sum(jnp.where(eye, row, 0.0), axis=1, keepdims=True)
                tcol[pl.ds(((cc * NX + xx) * NY + yy) * SEQ, SEQ), :] = col

    @pl.loop(1, WAVES + 6)
    def _(i):
        @pl.when(i < WAVES)
        def _():
            z_in(i)
            z_on(i)
            s1(hab, slot(i), wa, i)

        @pl.when(i == 1)
        def _():
            s2(hc, z, wc, LAST)

        @pl.when((i >= 1) & (i < WAVES + 1))
        def _():
            s2(hab, slot(i - 1), wa, i - 1)

        @pl.when(i == 2)
        def _():
            s3(hc, z, wc, LAST)

        @pl.when((i >= 2) & (i < WAVES + 2))
        def _():
            s3(hab, slot(i - 2), wa, i - 2)

        @pl.when(i == 3)
        def _():
            s4(hc, z, wc, LAST)

        @pl.when((i >= 3) & (i < WAVES + 3))
        def _():
            s4(hab, slot(i - 3), wa, i - 3)

        @pl.when(i == 4)
        def _():
            s5(hc, z, wc, LAST)
            t1()
            thin_over(0)
            for k in range(NZ):
                weights(k).wait()

        @pl.when((i >= 4) & (i < WAVES + 4))
        def _():
            j = i - 4
            s5(hab, slot(j), wa, j)
            push(hab.at[slot(j), c], ds.at[j], dr.at[j], partner)

        @pl.when(i == 5)
        def _():
            t_step(1, 0)
            thin_multiply(0)

        @pl.when((i >= 5) & (i < WAVES + 5))
        def _():
            j = i - 5
            got(hab.at[0, 0], ds.at[j], dr.at[j])
            multiply(hab, slot(j), 0, WIDE)

        @pl.when(i == 6)
        def _():
            t_step(1, 1)
            thin_over(1)

        @pl.when(i == 7)
        def _():
            t_step(2, 0)
            thin_multiply(1)

        @pl.when(i == 8)
        def _():
            t_step(2, 1)
            thin_over(2)

        @pl.when(i == 9)
        def _():
            t_step(3, 0)
            thin_multiply(2)

        @pl.when(i == 10)
        def _():
            t_step(3, 1)
            thin_over(3)

        @pl.when(i == 11)
        def _():
            thin_multiply(3)

        @pl.when(i == 12)
        def _():
            t_in(4, 0)
            thin_over(4)
            thin_multiply(4)

    offset = (((aa * NX + x) * NZ + z) * vocab).astype(F32)
    lane = lax.broadcasted_iota(jnp.int32, (128, vocab), 1).astype(F32) + offset
    which = lax.broadcasted_iota(jnp.int32, (128, 128), 1)

    @pl.loop(0, NC * NX)
    def _(r):
        rows = pl.ds(pl.multiple_of(r * 128, 128), 128)
        logits = acc[rows, :]
        top = jnp.max(logits, axis=1, keepdims=True)
        total = jnp.sum(jnp.exp(logits - top), axis=1, keepdims=True)
        picked = jnp.sum(jnp.where(lane == tcol[rows, :], logits, 0.0), axis=1, keepdims=True)
        packed = jnp.where(which == 0, top, jnp.where(which == 1, total, jnp.where(which == 2, picked, 0.0)))
        stat[r] = packed.T[0:8]

    def merged(ref):
        tops, totals, picks = ref[:, 0:1, :], ref[:, 1:2, :], ref[:, 2:3, :]
        top = jnp.max(tops, axis=0)
        total = jnp.sum(jnp.exp(tops - top[None]) * totals, axis=0)
        return top, total, jnp.sum(picks, axis=0)

    me = (c * NX + x) * NY + y
    for n in range(1, NC * NX * NY):
        peer = (me + n) % (NC * NX * NY)
        group, py = peer // NY, peer % NY
        copy(stat.at[group], gath.at[me], es.at[0], er.at[0],
             at(group % NX, py, z, group // NX)).start()
    gath[me] = stat[c * NX + x]
    got(gath.at[pl.ds(0, NC * NX * NY - 1)], es.at[0], er.at[0])
    top, total, picked = merged(gath)
    zst[z] = jnp.concatenate([top, total, picked, jnp.zeros((5, 128), F32)], axis=0)
    for n in range(1, NZ):
        push(zst.at[z], es.at[1], er.at[1], at(x, y, (z + n) % NZ, c))
    got(zst.at[pl.ds(0, NZ - 1)], es.at[1], er.at[1])
    top, total, picked = merged(zst)
    logprob = picked - top - jnp.log(total)
    length = lengths[aa, x]
    spot = lax.broadcasted_iota(jnp.int32, (1, 128), 1) - y * SEQ
    live = (spot >= 0) & (spot < length)
    out[...] = jnp.sum(jnp.where(live, logprob, 0.0), axis=1, keepdims=True) / length.astype(F32)

    @pl.loop(0, WAVES)
    def _(j):
        s_done(hab, wa, j)
        sent(hab.at[0, 0], ds.at[j], dr.at[j])

        @pl.when(j > 0)
        def _():
            sent(hab.at[0, 0, 0, 0], zs.at[j], zr.at[j])

    s_done(hc, wc, LAST)
    for k in range(3):
        for q in range(2):
            sent(hc.at[0, 0], ts.at[k, q], tr.at[k, q])
    sent(hc.at[0, 0], ts.at[3, 0], tr.at[3, 0])
    for k in range(5):
        sent(thin_bytes(k), cs.at[k], cr.at[k])
    sent(gath.at[pl.ds(0, NC * NX * NY - 1)], es.at[0], er.at[0])
    sent(zst.at[pl.ds(0, NZ - 1)], es.at[1], er.at[1])


def body(hidden, unembed, targets, lengths):
    depth, vocab = unembed.shape
    rows = NC * NX * NY * SEQ
    dma = pltpu.SemaphoreType.DMA
    return pl.pallas_call(
        kernel,
        out_shape=jax.ShapeDtypeStruct((1, 1), F32),
        in_specs=[
            pl.BlockSpec(memory_space=pl.ANY),
            pl.BlockSpec(memory_space=pl.ANY),
            pl.BlockSpec(memory_space=pltpu.VMEM),
            pl.BlockSpec(memory_space=pltpu.SMEM),
        ],
        out_specs=pl.BlockSpec(memory_space=pltpu.VMEM),
        scratch_shapes=[
            pltpu.VMEM((NZ, NC, NX, NY, SEQ, WIDE), BF16),
            pltpu.VMEM((NZ, NC, NX, NY, SEQ, THIN), BF16),
            pltpu.VMEM((NZ, depth // NZ, vocab), BF16),
            pltpu.VMEM((rows, vocab), F32),
            pltpu.VMEM((rows, 1), F32),
            pltpu.VMEM((NC * NX, 8, 128), F32),
            pltpu.VMEM((NC * NX * NY, 8, 128), F32),
            pltpu.VMEM((NZ, 8, 128), F32),
            dma((2,)), dma((NZ,)),
            dma((WAVES,)), dma((WAVES,)),
            dma((WAVES + 1, 4)), dma((WAVES + 1, 4)),
            dma((4, 2)), dma((4, 2)),
            dma((WAVES,)), dma((WAVES,)),
            dma((5,)), dma((5,)),
            dma((2,)), dma((2,)),
        ],
        compiler_params=pltpu.CompilerParams(
            collective_id=0, has_side_effects=True, vmem_limit_bytes=60 << 20
        ),
    )(hidden, unembed, targets, lengths)


def solution(mesh):
    assert dict(mesh.shape) == {"aa": NY * NC, "ba": NX, "col": NZ}
    in_specs = (P("aa", "ba", None, "col"), P(None, ("aa", "ba", "col")), P(), P())
    return jax.shard_map(body, mesh=mesh, in_specs=in_specs, out_specs=P("aa", "ba"), check_vma=False)
```

time: 186 us -> 95.5 us (0.51)
  the two profiles are of different devices: /device:TPU:2 before, /device:TPU:1 now
where the time goes in v1:
time: 95.5 us; the launch traced here: 94.9 us
  Pallas kernels  78.4 us (82%)
  local copies, waits for them, and re-layouts  15.5 us (16%)
  between operations  1.06 us (1%)
    pallas_call x1, Pallas kernels, body(): pl.pallas_call(kernel, out_shape=jax.ShapeDtypeStruct((1, 1), F32), in_sp...  78.4 us
    unnamed x2, local copies, waits for them, and re-layouts  15.5 us

profile of v1, /device:TPU:1, one launch (start us, length us, event | category | flops | bytes accessed | tf_op | source)
XLA Modules:
  0.0 94.9 jit_solution(329905867233438583)
XLA Ops:
  0.0 1.3 %copy.6.lengths = s32[8,4]{1,0:T(8,128)} copy(s32[8,4]{0,1:T(4,128)} %param.7) | data formatting | bytes 256 | tf_op args[3]
  1.3 14.2 %copy.5.unembed = bf16[8192,594]{1,0:T(8,128)(2,1)} copy(bf16[8192,594]{0,1:T(8,128)(2,1)} %param.5) | data formatting | bytes 19464192 | tf_op args[1]
  15.5 78.4 %shard_map.46 = f32[1,1]{1,0:T(1,128)} custom-call(bf16[1,1,32,1024]{3,2,1,0:T(8,128)(2,1)} %hid.1, bf16[8192,594]{1,0:T(8,128)(2,1)} %copy.5.unembed, s32[8,4,32]{2,1,0:T(4,128)} %targets.1, s32[8,4]{1,0:T(8,128)} %copy.6.lengths), custom_call_target="tpu_custom_call" | custom-call | tf_op jit(solution)/shard_map/pallas_call | solution.py:352
